TPU v7x, 64 devices: a 2x2x8 block of a 4x4x8 slice. The times are simulated.
64 devices in a mesh: data: 4 (over x, y), seq: 16 (over z, core).
Axes of the slice: x: 2, y: 2, z: 8, core: 2. Of those that a mesh axis runs over, the one named last changes fastest.
The devices are a block of a 4x4x8 slice.
Arguments:
- x: bfloat16 [16384, 1024], P(('data', 'seq')), parts along dimension 0
- g1: float32 [1024], replicated
- b1: float32 [1024], replicated
- g2: float32 [1024], replicated
- b2: float32 [1024], replicated
- wqkv: bfloat16 [1024, 3072], replicated
- wo: bfloat16 [16, 64, 1024], replicated
- w1: bfloat16 [1024, 4096], replicated
- w2: bfloat16 [4096, 1024], replicated
Outputs:
- output: bfloat16 [16384, 1024], P(('data', 'seq')), parts along dimension 0
There are 4 independent parts. A program takes and returns all parts, laid end to end along the dimension named above; an argument that names none is the same for every part.
All inputs are finite; a program needn't handle non-finite values.
Results may differ from a plain program's by a relative error of at most 0.00216896.
Values are sent between devices in bfloat16 or wider.
A program may use at most 768 MiB of HBM per device.

v0:
```python
import functools
import math

import jax
import jax.numpy as jnp
from jax import lax
from jax.experimental import pallas as pl
from jax.experimental.pallas import tpu as pltpu
from jax.sharding import PartitionSpec as P

EPS = 1e-5
NEG = -1e30
F32 = jnp.float32
BF16 = jnp.bfloat16
LANES = 128
HCOL = 512


def _roll(t, shift):
    return pltpu.roll(t, shift, 1)


def _low(shape):
    return lax.broadcasted_iota(jnp.int32, shape, 1) < LANES // 2


def _pair(top, bot):
    low = _low(top.shape)
    return jnp.where(low, top, _roll(bot, LANES // 2)), jnp.where(low, _roll(top, LANES // 2), bot)


def _kernel(n, x_ref, g1_ref, b1_ref, g2_ref, b2_ref, cos_ref, sin_ref, wqkv_ref, wo_ref, w1_ref, w2_ref, y_ref,
            wq_v, wo_v, w1_v, w2_v, a_v, m_v, acc_v, send, recv, s_v, o_send, o_recv, o_v,
            wq_sem, wo_sem, w1_sem, w2_sem, send_sem, recv_sem, osend_sem, orecv_sem):
    r, d = x_ref.shape
    half = r // 2
    chips = n // 2
    ngrp = n // 4
    gcol = d // ngrp
    nm = w1_v.shape[0]
    me = lax.axis_index("seq")
    chip, core = me // 2, me % 2
    g0 = ((chip + chips // 2) % chips) // 2

    barrier = pltpu.get_barrier_semaphore()

    def greet(i, _):
        pl.semaphore_signal(barrier, inc=1, device_id={"seq": (me + i) % n})
        return 0

    lax.fori_loop(1, n, greet, 0)

    def wq_copy(s, t):
        col = pl.multiple_of(t * d + ((g0 + s) % ngrp) * gcol, gcol)
        return pltpu.make_async_copy(wqkv_ref.at[:, pl.ds(col, gcol)], wq_v.at[s, t], wq_sem.at[s, t])

    def w1_copy(i):
        return pltpu.make_async_copy(w1_ref.at[:, pl.ds(pl.multiple_of(i * HCOL, HCOL), HCOL)], w1_v.at[i], w1_sem.at[i])

    def w2_copy(i):
        return pltpu.make_async_copy(w2_ref.at[pl.ds(pl.multiple_of(i * HCOL, HCOL), HCOL), :], w2_v.at[i], w2_sem.at[i])

    wo_copy = pltpu.make_async_copy(wo_ref, wo_v, wo_sem)

    for s in range(ngrp):
        for t in range(3):
            wq_copy(s, t).start()

    xf = x_ref[...].astype(F32)
    mu = jnp.mean(xf, axis=-1, keepdims=True)
    xc = xf - mu
    var = jnp.mean(jnp.square(xc), axis=-1, keepdims=True)
    xn = xc * lax.rsqrt(var + EPS)
    a_v[...] = (xn * g1_ref[...] + b1_ref[...]).astype(BF16)
    m_v[...] = (xn * g2_ref[...] + b2_ref[...]).astype(BF16)
    acc_v[...] = xf
    pl.semaphore_wait(barrier, n - 1)

    def rope(t):
        t = t.astype(BF16).astype(F32)
        lane = lax.broadcasted_iota(jnp.int32, t.shape, 1)
        partner = jnp.where(lane % 64 < 32, _roll(t, LANES - 32), _roll(t, 32))
        return t * cos_ref[...] + partner * sin_ref[...]

    def ship(dst, src, land, ssem, rsem):
        @pl.when(dst == me)
        def _():
            pltpu.make_async_copy(src.at[dst], land.at[me], rsem.at[me]).start()

        @pl.when(dst != me)
        def _():
            pltpu.make_async_remote_copy(
                src_ref=src.at[dst], dst_ref=land.at[me], send_sem=ssem.at[dst], recv_sem=rsem.at[me],
                device_id={"seq": dst}).start()

    def qkv_step(s, _):
        g = (g0 + s) % ngrp
        for t in range(3):
            wq_copy(s, t).wait()
        for i in range(nm // ngrp):
            w1_copy(s * (nm // ngrp) + i).start()
            w2_copy(s * (nm // ngrp) + i).start()
        a = a_v[...]
        q, k, v = (jnp.dot(a, wq_v[s, t], preferred_element_type=F32) for t in range(3))
        for j in range(2):
            cols = slice(j * LANES, (j + 1) * LANES)
            qr, kr, vr = rope(q[:, cols]), rope(k[:, cols]), v[:, cols]
            kv = _pair(kr, vr)
            qq = _pair(qr[:half], qr[half:])
            for e in range(2):
                send[4 * g + 2 * j + e, :r, :] = kv[e].astype(BF16)
                send[4 * g + 2 * j + e, r:, :] = qq[e].astype(BF16)
        for i in range(4):
            ship(4 * g + i, send, recv, send_sem, recv_sem)
        return 0

    lax.fori_loop(0, ngrp, qkv_step, 0)
    wo_copy.start()

    def mlp_step(i, _):
        w1_copy(i).wait()
        w2_copy(i).wait()

        u = jnp.dot(m_v[...], w1_v[i], preferred_element_type=F32)
        h = (0.5 * u * (1.0 + lax.erf(u * (0.5 ** 0.5)))).astype(BF16)
        acc_v[...] += jnp.dot(h, w2_v[i], preferred_element_type=F32)
        return 0

    lax.fori_loop(0, nm, mlp_step, 0)

    def arrived(i, _):
        pltpu.make_async_copy(send.at[i], recv.at[i], recv_sem.at[i]).wait()
        return 0

    lax.fori_loop(0, n, arrived, 0)

    scale = 64.0 ** -0.5 * math.log2(math.e)

    def attend(s, _):
        i = s // 2
        off = chips // 2 + ((i + 1) // 2) * (1 - 2 * (i % 2))
        qi = ((chip + off) % chips) * 2 + (core + 1 + s) % 2
        qp = recv[qi, r:, :].astype(F32)
        low = _low(qp.shape)
        q = jnp.concatenate([jnp.where(low, qp, 0.0), jnp.where(low, _roll(qp, LANES // 2), 0.0)], axis=0).astype(BF16)

        def scores(b):
            return lax.dot_general(q, recv[b, :r, :], (((1,), (1,)), ((), ())), preferred_element_type=F32)

        def top(sc):
            out = sc[:, :LANES]
            for c in range(1, sc.shape[1] // LANES):
                out = jnp.maximum(out, sc[:, c * LANES:(c + 1) * LANES])
            return out

        def first(t, mx):
            for u in range(2):
                sc = scores(2 * t + u)
                s_v[2 * t + u] = sc
                mx = jnp.maximum(mx, top(sc))
            return mx

        nfull = qi // 2
        mx = lax.fori_loop(0, nfull, first, jnp.full((r, LANES), NEG, F32))
        for u in range(2):
            b = 2 * nfull + u
            sc = scores(b)
            rows = qi * r + lax.broadcasted_iota(jnp.int32, sc.shape, 0)
            cols = b * r + lax.broadcasted_iota(jnp.int32, sc.shape, 1)
            sc = jnp.where(cols <= rows, sc, NEG)
            s_v[b] = sc
            mx = jnp.maximum(mx, top(sc))
        mx = jnp.max(mx, axis=1, keepdims=True) * scale

        def second(t, carry):
            den, out = carry
            for u in range(2):
                p = jnp.exp2(s_v[2 * t + u] * scale - mx)
                for c in range(r // LANES):
                    den = den + p[:, c * LANES:(c + 1) * LANES]
                out = out + jnp.dot(p.astype(BF16), recv[2 * t + u, :r, :], preferred_element_type=F32)
            return den, out

        zero = jnp.zeros((r, LANES), F32)
        den, out = lax.fori_loop(0, nfull + 1, second, (zero, zero))
        out = out / jnp.sum(den, axis=1, keepdims=True)
        o_send[qi] = _pair(out[:half], out[half:])[1].astype(BF16)
        ship(qi, o_send, o_recv, osend_sem, orecv_sem)
        return 0

    lax.fori_loop(0, n, attend, 0)

    def returned(i, _):
        pltpu.make_async_copy(o_send.at[i], o_recv.at[i], orecv_sem.at[i]).wait()
        return 0

    lax.fori_loop(0, n, returned, 0)
    for c in range(n // 2):
        p0, p1 = o_recv[2 * c].astype(F32), o_recv[2 * c + 1].astype(F32)
        t, b = _pair(p0, p1)
        o_v[:half, c * LANES:(c + 1) * LANES] = t.astype(BF16)
        o_v[half:, c * LANES:(c + 1) * LANES] = b.astype(BF16)
    wo_copy.wait()
    for c in range(d // 256):
        cols = slice(c * 256, (c + 1) * 256)
        y_ref[:, cols] = (acc_v[:, cols] + jnp.dot(o_v[...], wo_v[:, cols], preferred_element_type=F32)).astype(BF16)

    def drained(i, _):
        @pl.when(i != me)
        def _():
            for buf, land, sem in ((send, recv, send_sem), (o_send, o_recv, osend_sem)):
                pltpu.make_async_copy(buf.at[0], land.at[0], sem.at[i]).wait()
        return 0

    lax.fori_loop(0, n, drained, 0)


def _tables(pos, dh):
    half = dh // 2
    inv = 10000.0 ** (-2.0 * jnp.arange(half, dtype=F32) / dh)
    ang = pos.astype(F32)[:, None] * inv[None, :]
    cos, sin = jnp.cos(ang), jnp.sin(ang)
    return jnp.concatenate([cos] * 4, axis=1), jnp.concatenate([-sin, sin, -sin, sin], axis=1)


def solution(mesh):
    n = mesh.shape["seq"]

    def local(x, g1, b1, g2, b2, wqkv, wo, w1, w2):
        r, d = x.shape
        nh, dh, _ = wo.shape
        f = w1.shape[1]
        assert nh == n and dh * 2 == LANES and r == 256
        cos, sin = _tables(lax.axis_index("seq") * r + jnp.arange(r), dh)
        nm, ngrp, chunk = f // HCOL, n // 4, r + r // 2
        vm = pl.BlockSpec(memory_space=pltpu.VMEM)
        hbm = pl.BlockSpec(memory_space=pl.ANY)
        dma = pltpu.SemaphoreType.DMA
        return pl.pallas_call(
            functools.partial(_kernel, n),
            out_shape=jax.ShapeDtypeStruct((r, d), BF16),
            in_specs=[vm] * 7 + [hbm] * 4,
            out_specs=vm,
            scratch_shapes=[
                pltpu.VMEM((ngrp, 3, d, d // ngrp), BF16), pltpu.VMEM((d, d), BF16),
                pltpu.VMEM((nm, d, HCOL), BF16), pltpu.VMEM((nm, HCOL, d), BF16),
                pltpu.VMEM((r, d), BF16), pltpu.VMEM((r, d), BF16), pltpu.VMEM((r, d), F32),
                pltpu.VMEM((n, chunk, LANES), BF16), pltpu.VMEM((n, chunk, LANES), BF16),
                pltpu.VMEM((n, r, r), F32),
                pltpu.VMEM((n, r // 2, LANES), BF16), pltpu.VMEM((n, r // 2, LANES), BF16),
                pltpu.VMEM((r, d), BF16),
                dma((ngrp, 3)), dma, dma((nm,)), dma((nm,)),
                dma((n,)), dma((n,)), dma((n,)), dma((n,)),
            ],
            compiler_params=pltpu.CompilerParams(
                collective_id=0, has_side_effects=True, vmem_limit_bytes=62 * 2 ** 20),
            name="layer",
        )(x, g1[None], b1[None], g2[None], b2[None], cos, sin, wqkv, wo.reshape(nh * dh, d), w1, w2)

    rows = P(("data", "seq"), None)
    rep = P()
    return jax.shard_map(local, mesh=mesh,
                         in_specs=(rows, rep, rep, rep, rep, rep, rep, rep, rep),
                         out_specs=rows, check_vma=False)
```

profile of v0, /device:TPU:21, one launch (start us, length us, event | category | flops | bytes accessed | tf_op | source)
XLA Modules:
  0.0 94.9 jit_solution(11016125292186321048)
XLA Ops:
  0.0 0.5 fusion
  0.6 1.0 %pad_maximum_fusion = (f32[256,128]{1,0:T(8,128)}, f32[256,128]{1,0:T(8,128)}) fusion(f32[256,32]{1,0:T(8,128)S(1)} %get-tuple-element.7, f32[256,32]{1,0:T(8,128)S(1)} %get-tuple-element.6, f32[256,32]{1,0:T(8,128)S(1)} %get-tuple-element.5), kind=kLoop, calls=%fused_computation.2 | loop fusion | flops 196608 | bytes 360448 | tf_op jit(solution)/shard_map/concatenate | solution.py:223
  1.5 91.5 %layer.1 = bf16[256,1024]{1,0:T(8,128)(2,1)} custom-call(bf16[256,1024]{1,0:T(8,128)(2,1)} %x_ref.1, f32[1,1024]{1,0:T(1,128)} %bitcast.6, f32[1,1024]{1,0:T(1,128)} %bitcast.7, f32[1,1024]{1,0:T(1,128)} %bitcast.8, f32[1,1024]{1,0:T(1,128)} %bitcast.9, f32[256,128]{1,0:T(8,128)} %get-tuple-element.8.cos_ref, f32[256,128]{1,0:T(8,128)} %get-tuple-element.9.sin_ref, ...), custom_call_target="tpu_custom_call" | custom-call | tf_op jit(solution)/shard_map/layer/pallas_call | solution.py:239
  93.0 1.9 %copy.12 = bf16[256,1024]{1,0:T(8,128)(2,1)} copy(bf16[256,1024]{1,0:T(8,128)(2,1)} %layer.1) | data formatting | bytes 1048576
  (2 shorter events, 0.0 us)
where the time goes:
time: 95 us; the launch traced here: 94.9 us
  Pallas kernels  91.5 us (96%)
  local copies, waits for them, and re-layouts  1.87 us (2%)
  other arithmetic  1.52 us (2%)
    pallas_call x1, Pallas kernels, local(): pl.pallas_call(functools.partial(_kernel, n), out_shape=jax.ShapeDtypeStr...  91.5 us

commit v1 on v0

--- a/solution.py
+++ b/solution.py
@@ -29,18 +29,22 @@
     return jnp.where(low, top, _roll(bot, LANES // 2)), jnp.where(low, _roll(top, LANES // 2), bot)
 
 
-def _kernel(n, x_ref, g1_ref, b1_ref, g2_ref, b2_ref, cos_ref, sin_ref, wqkv_ref, wo_ref, w1_ref, w2_ref, y_ref,
-            wq_v, wo_v, w1_v, w2_v, a_v, m_v, acc_v, send, recv, s_v, o_send, o_recv, o_v,
+def _transposed(t):
+    return t.reshape(t.shape[0] // 8, 8, t.shape[1])
+
+
+def _kernel(n, scale, x_ref, g1_ref, b1_ref, g2_ref, b2_ref, cos_ref, sin_ref, wqkv_ref, wo_ref, w1_ref, w2_ref, y_ref,
+            wq_v, wo_v, w1_v, w2_v, a_v, m_v, acc_v, send, recv, qp_v, s_v, top_v, den_v, out_v, o_send, o_recv, o_v,
             wq_sem, wo_sem, w1_sem, w2_sem, send_sem, recv_sem, osend_sem, orecv_sem):
     r, d = x_ref.shape
-    half = r // 2
+    dh = LANES // 2
     chips = n // 2
     ngrp = n // 4
     gcol = d // ngrp
     nm = w1_v.shape[0]
     me = lax.axis_index("seq")
     chip, core = me // 2, me % 2
-    g0 = ((chip + chips // 2) % chips) // 2
+    odd = chip % 2
 
     barrier = pltpu.get_barrier_semaphore()
 
@@ -50,8 +54,11 @@
 
     lax.fori_loop(1, n, greet, 0)
 
+    def group(s):
+        return (chip // 2 + jnp.where(s == 0, 0, jnp.where(s == 1, 1, jnp.where(s == 2, ngrp - 1, 2)))) % ngrp
+
     def wq_copy(s, t):
-        col = pl.multiple_of(t * d + ((g0 + s) % ngrp) * gcol, gcol)
+        col = pl.multiple_of(t * d + group(s) * gcol, gcol)
         return pltpu.make_async_copy(wqkv_ref.at[:, pl.ds(col, gcol)], wq_v.at[s, t], wq_sem.at[s, t])
 
     def w1_copy(i):
@@ -94,7 +101,7 @@
                 device_id={"seq": dst}).start()
 
     def qkv_step(s, _):
-        g = (g0 + s) % ngrp
+        g = group(s)
         for t in range(3):
             wq_copy(s, t).wait()
         for i in range(nm // ngrp):
@@ -102,16 +109,18 @@
             w2_copy(s * (nm // ngrp) + i).start()
         a = a_v[...]
         q, k, v = (jnp.dot(a, wq_v[s, t], preferred_element_type=F32) for t in range(3))
+        vt = v.T.astype(BF16)
         for j in range(2):
             cols = slice(j * LANES, (j + 1) * LANES)
-            qr, kr, vr = rope(q[:, cols]), rope(k[:, cols]), v[:, cols]
-            kv = _pair(kr, vr)
-            qq = _pair(qr[:half], qr[half:])
+            kq = _pair(rope(k[:, cols]), rope(q[:, cols]))
             for e in range(2):
-                send[4 * g + 2 * j + e, :r, :] = kv[e].astype(BF16)
-                send[4 * g + 2 * j + e, r:, :] = qq[e].astype(BF16)
+                h = 2 * j + e
+                send[4 * g + h, :r, :] = kq[e].astype(BF16)
+                for c in range(r // LANES):
+                    send[4 * g + h, r + c * dh:r + (c + 1) * dh, :] = vt[h * dh:(h + 1) * dh, c * LANES:(c + 1) * LANES]
+        near = jnp.where(s == 0, odd, jnp.where(s == 1, 0, jnp.where(s == 2, 1, 1 - odd)))
         for i in range(4):
-            ship(4 * g + i, send, recv, send_sem, recv_sem)
+            ship(4 * g + 2 * (near + i // 2 - 2 * near * (i // 2)) + i % 2, send, recv, send_sem, recv_sem)
         return 0
 
     lax.fori_loop(0, ngrp, qkv_step, 0)
@@ -120,7 +129,6 @@
     def mlp_step(i, _):
         w1_copy(i).wait()
         w2_copy(i).wait()
-
         u = jnp.dot(m_v[...], w1_v[i], preferred_element_type=F32)
         h = (0.5 * u * (1.0 + lax.erf(u * (0.5 ** 0.5)))).astype(BF16)
         acc_v[...] += jnp.dot(h, w2_v[i], preferred_element_type=F32)
@@ -128,78 +136,98 @@
 
     lax.fori_loop(0, nm, mlp_step, 0)
 
-    def arrived(i, _):
-        pltpu.make_async_copy(send.at[i], recv.at[i], recv_sem.at[i]).wait()
-        return 0
-
-    lax.fori_loop(0, n, arrived, 0)
-
-    scale = 64.0 ** -0.5 * math.log2(math.e)
-
-    def attend(s, _):
-        i = s // 2
-        off = chips // 2 + ((i + 1) // 2) * (1 - 2 * (i % 2))
-        qi = ((chip + off) % chips) * 2 + (core + 1 + s) % 2
-        qp = recv[qi, r:, :].astype(F32)
-        low = _low(qp.shape)
-        q = jnp.concatenate([jnp.where(low, qp, 0.0), jnp.where(low, _roll(qp, LANES // 2), 0.0)], axis=0).astype(BF16)
-
-        def scores(b):
-            return lax.dot_general(q, recv[b, :r, :], (((1,), (1,)), ((), ())), preferred_element_type=F32)
-
-        def top(sc):
-            out = sc[:, :LANES]
-            for c in range(1, sc.shape[1] // LANES):
-                out = jnp.maximum(out, sc[:, c * LANES:(c + 1) * LANES])
-            return out
-
-        def first(t, mx):
-            for u in range(2):
-                sc = scores(2 * t + u)
-                s_v[2 * t + u] = sc
-                mx = jnp.maximum(mx, top(sc))
-            return mx
-
-        nfull = qi // 2
-        mx = lax.fori_loop(0, nfull, first, jnp.full((r, LANES), NEG, F32))
-        for u in range(2):
-            b = 2 * nfull + u
-            sc = scores(b)
-            rows = qi * r + lax.broadcasted_iota(jnp.int32, sc.shape, 0)
-            cols = b * r + lax.broadcasted_iota(jnp.int32, sc.shape, 1)
-            sc = jnp.where(cols <= rows, sc, NEG)
-            s_v[b] = sc
-            mx = jnp.maximum(mx, top(sc))
-        mx = jnp.max(mx, axis=1, keepdims=True) * scale
-
-        def second(t, carry):
-            den, out = carry
-            for u in range(2):
-                p = jnp.exp2(s_v[2 * t + u] * scale - mx)
-                for c in range(r // LANES):
-                    den = den + p[:, c * LANES:(c + 1) * LANES]
-                out = out + jnp.dot(p.astype(BF16), recv[2 * t + u, :r, :], preferred_element_type=F32)
-            return den, out
-
-        zero = jnp.zeros((r, LANES), F32)
-        den, out = lax.fori_loop(0, nfull + 1, second, (zero, zero))
-        out = out / jnp.sum(den, axis=1, keepdims=True)
-        o_send[qi] = _pair(out[:half], out[half:])[1].astype(BF16)
-        ship(qi, o_send, o_recv, osend_sem, orecv_sem)
-        return 0
-
-    lax.fori_loop(0, n, attend, 0)
+    def order(t):
+        return (chip + jnp.where(t % 2 == 1, (t + 1) // 2, chips - t // 2)) % chips
+
+    def place(c):
+        away = (c + chips - chip) % chips
+        return jnp.where(away == 0, 0, jnp.where(away <= chips // 2, 2 * away - 1, 2 * (chips - away)))
+
+    def ready(i):
+        last = place(i)
+        for j in range(chips):
+            last = jnp.where(j <= i, jnp.maximum(last, place(j)), last)
+        return last
+
+    def job(i, j, diag):
+        for h in range(2):
+            qi = 2 * i + h
+            halves = range(h + 1) if diag else range(2)
+            top = None
+            for g in halves:
+                sc = lax.dot_general(recv[2 * j + g, :r, :], qp_v[qi], (((1,), (1,)), ((), ())),
+                                     preferred_element_type=F32)
+                if diag and g == h:
+                    key = lax.broadcasted_iota(jnp.int32, sc.shape, 0)
+                    row = lax.broadcasted_iota(jnp.int32, sc.shape, 1)
+                    sc = jnp.where(key <= row, sc, NEG)
+                s_v[h, g] = sc
+                part = jnp.max(_transposed(sc), axis=0)
+                top = part if top is None else jnp.maximum(top, part)
+            top = jnp.max(top, axis=0, keepdims=True)
+            if not diag:
+                old = top_v[qi]
+                top = jnp.maximum(top, old)
+                alpha = jnp.exp2((old - top) * scale)
+            top_v[qi] = top
+            den, out = None, None
+            for g in halves:
+                p = jnp.exp2(s_v[h, g] * scale - top * scale)
+                part = jnp.sum(_transposed(p), axis=0)
+                den = part if den is None else den + part
+                vt = jnp.concatenate([recv[2 * j + g, r + c * dh:r + (c + 1) * dh, :] for c in range(r // LANES)], axis=1)
+                part = jnp.dot(vt, p.astype(BF16), preferred_element_type=F32)
+                out = part if out is None else out + part
+            if not diag:
+                den = den_v[qi] * alpha + den
+                out = out_v[qi] * alpha + out
+            den_v[qi] = den
+            out_v[qi] = out
+
+    def finish(i):
+        for h in range(2):
+            qi = 2 * i + h
+            o = (out_v[qi] / jnp.sum(den_v[qi], axis=0, keepdims=True)).astype(BF16)
+            for c in range(r // LANES):
+                o_send[qi, c * dh:(c + 1) * dh, :] = o[:, c * LANES:(c + 1) * LANES]
+        for h in range(2):
+            ship(2 * i + h, o_send, o_recv, osend_sem, orecv_sem)
+
+    def attend(t, _):
+        b = order(t)
+        for h in range(2):
+            pltpu.make_async_copy(send.at[2 * b + h], recv.at[2 * b + h], recv_sem.at[2 * b + h]).wait()
+            kq = recv[2 * b + h, :r, :].astype(F32)
+            qp_v[2 * b + h] = jnp.where(_low(kq.shape), _roll(kq, dh), 0.0).astype(BF16)
+        job(b, b, True)
+
+        def pairs(u, _):
+            c = order(t - 1 - u)
+            i = jnp.maximum(b, c)
+            job(i, jnp.minimum(b, c), False)
+
+            @pl.when((i != b) & (ready(i) == t))
+            def _():
+                finish(i)
+            return 0
+
+        lax.fori_loop(0, t, pairs, 0)
+
+        @pl.when(ready(b) == t)
+        def _():
+            finish(b)
+        return 0
+
+    lax.fori_loop(0, chips, attend, 0)
 
     def returned(i, _):
         pltpu.make_async_copy(o_send.at[i], o_recv.at[i], orecv_sem.at[i]).wait()
         return 0
 
     lax.fori_loop(0, n, returned, 0)
-    for c in range(n // 2):
-        p0, p1 = o_recv[2 * c].astype(F32), o_recv[2 * c + 1].astype(F32)
-        t, b = _pair(p0, p1)
-        o_v[:half, c * LANES:(c + 1) * LANES] = t.astype(BF16)
-        o_v[half:, c * LANES:(c + 1) * LANES] = b.astype(BF16)
+    for c in range(r // LANES):
+        ot = o_recv[:, c * dh:(c + 1) * dh, :].reshape(n * dh, LANES)
+        o_v[c * LANES:(c + 1) * LANES, :] = ot.T
     wo_copy.wait()
     for c in range(d // 256):
         cols = slice(c * 256, (c + 1) * 256)
@@ -237,7 +265,7 @@
         hbm = pl.BlockSpec(memory_space=pl.ANY)
         dma = pltpu.SemaphoreType.DMA
         return pl.pallas_call(
-            functools.partial(_kernel, n),
+            functools.partial(_kernel, n, dh ** -0.5 * math.log2(math.e)),
             out_shape=jax.ShapeDtypeStruct((r, d), BF16),
             in_specs=[vm] * 7 + [hbm] * 4,
             out_specs=vm,
@@ -246,7 +274,8 @@
                 pltpu.VMEM((nm, d, HCOL), BF16), pltpu.VMEM((nm, HCOL, d), BF16),
                 pltpu.VMEM((r, d), BF16), pltpu.VMEM((r, d), BF16), pltpu.VMEM((r, d), F32),
                 pltpu.VMEM((n, chunk, LANES), BF16), pltpu.VMEM((n, chunk, LANES), BF16),
-                pltpu.VMEM((n, r, r), F32),
+                pltpu.VMEM((n, r, LANES), BF16), pltpu.VMEM((2, 2, r, r), F32),
+                pltpu.VMEM((n, 1, r), F32), pltpu.VMEM((n, 8, r), F32), pltpu.VMEM((n, dh, r), F32),
                 pltpu.VMEM((n, r // 2, LANES), BF16), pltpu.VMEM((n, r // 2, LANES), BF16),
                 pltpu.VMEM((r, d), BF16),
                 dma((ngrp, 3)), dma, dma((nm,)), dma((nm,)),

time: 95 us -> 75.5 us (0.79)
  the two profiles are of different devices: /device:TPU:21 before, /device:TPU:127 now
where the time goes in v1:
time: 75.5 us; the launch traced here: 75.4 us
  Pallas kernels  72 us (95%)
  local copies, waits for them, and re-layouts  1.87 us (2%)
  other arithmetic  1.52 us (2%)
    pallas_call x1, Pallas kernels, local(): pl.pallas_call(functools.partial(_kernel, n, dh ** (-0.5) * math.log2(mat...  72 us
    unnamed x1, local copies, waits for them, and re-layouts  1.87 us

profile of v1, /device:TPU:127, one launch (start us, length us, event | category | flops | bytes accessed | tf_op | source)
XLA Modules:
  0.0 75.4 jit_solution(4286411082734854548)
XLA Ops:
  0.0 0.5 fusion
  0.6 1.0 %pad_maximum_fusion = (f32[256,128]{1,0:T(8,128)}, f32[256,128]{1,0:T(8,128)}) fusion(f32[256,32]{1,0:T(8,128)S(1)} %get-tuple-element.7, f32[256,32]{1,0:T(8,128)S(1)} %get-tuple-element.6, f32[256,32]{1,0:T(8,128)S(1)} %get-tuple-element.5), kind=kLoop, calls=%fused_computation.2 | loop fusion | flops 196608 | bytes 360448 | tf_op jit(solution)/shard_map/concatenate | solution.py:251
  1.5 72.0 %layer.1 = bf16[256,1024]{1,0:T(8,128)(2,1)} custom-call(bf16[256,1024]{1,0:T(8,128)(2,1)} %x_ref.1, f32[1,1024]{1,0:T(1,128)} %bitcast.6, f32[1,1024]{1,0:T(1,128)} %bitcast.7, f32[1,1024]{1,0:T(1,128)} %bitcast.8, f32[1,1024]{1,0:T(1,128)} %bitcast.9, f32[256,128]{1,0:T(8,128)} %get-tuple-element.8.cos_ref, f32[256,128]{1,0:T(8,128)} %get-tuple-element.9.sin_ref, ...), custom_call_target="tpu_custom_call" | custom-call | tf_op jit(solution)/shard_map/layer/pallas_call | solution.py:267
  73.5 1.9 %copy.12 = bf16[256,1024]{1,0:T(8,128)(2,1)} copy(bf16[256,1024]{1,0:T(8,128)(2,1)} %layer.1) | data formatting | bytes 1048576
  (2 shorter events, 0.0 us)

commit v2 on v1

--- a/solution.py
+++ b/solution.py
@@ -2,6 +2,7 @@
 import math
 
 import jax
+import numpy as np
 import jax.numpy as jnp
 from jax import lax
 from jax.experimental import pallas as pl
@@ -33,11 +34,12 @@
     return t.reshape(t.shape[0] // 8, 8, t.shape[1])
 
 
-def _kernel(n, scale, x_ref, g1_ref, b1_ref, g2_ref, b2_ref, cos_ref, sin_ref, wqkv_ref, wo_ref, w1_ref, w2_ref, y_ref,
-            wq_v, wo_v, w1_v, w2_v, a_v, m_v, acc_v, send, recv, qp_v, s_v, top_v, den_v, out_v, o_send, o_recv, o_v,
+def _kernel(n, scale, x_ref, g1_ref, b1_ref, g2_ref, b2_ref, turn_ref, base_ref, wqkv_ref, wo_ref, w1_ref, w2_ref, y_ref,
+            x_v, gb_v, turn_v, base_v, rot_v, y_v, in_sem, y_sem, wq_v, wo_v, w1_v, w2_v, a_v, m_v, acc_v, send, recv, k_v, qt_v, s_v, top_v, den_v, out_v, o_send, o_recv, o_v,
             wq_sem, wo_sem, w1_sem, w2_sem, send_sem, recv_sem, osend_sem, orecv_sem):
-    r, d = x_ref.shape
+    r, d = x_v.shape
     dh = LANES // 2
+    half = r // 2
     chips = n // 2
     ngrp = n // 4
     gcol = d // ngrp
@@ -53,6 +55,11 @@
         return 0
 
     lax.fori_loop(1, n, greet, 0)
+    small = [(x_ref, x_v), (turn_ref, turn_v), (base_ref, base_v)]
+    small += [(ref, gb_v.at[i]) for i, ref in enumerate((g1_ref, b1_ref, g2_ref, b2_ref))]
+    small = [pltpu.make_async_copy(src, dst, in_sem.at[i]) for i, (src, dst) in enumerate(small)]
+    for copy in small:
+        copy.start()
 
     def group(s):
         return (chip // 2 + jnp.where(s == 0, 0, jnp.where(s == 1, 1, jnp.where(s == 2, ngrp - 1, 2)))) % ngrp
@@ -73,13 +80,18 @@
         for t in range(3):
             wq_copy(s, t).start()
 
-    xf = x_ref[...].astype(F32)
+    for copy in small:
+        copy.wait()
+    cb, sb = (base_v[i, pl.ds(me, 1), :] for i in range(2))
+    rot_v[0] = cb * turn_v[0] - sb * turn_v[1]
+    rot_v[1] = sb * turn_v[0] + cb * turn_v[1]
+    xf = x_v[...].astype(F32)
     mu = jnp.mean(xf, axis=-1, keepdims=True)
     xc = xf - mu
     var = jnp.mean(jnp.square(xc), axis=-1, keepdims=True)
     xn = xc * lax.rsqrt(var + EPS)
-    a_v[...] = (xn * g1_ref[...] + b1_ref[...]).astype(BF16)
-    m_v[...] = (xn * g2_ref[...] + b2_ref[...]).astype(BF16)
+    a_v[...] = (xn * gb_v[0] + gb_v[1]).astype(BF16)
+    m_v[...] = (xn * gb_v[2] + gb_v[3]).astype(BF16)
     acc_v[...] = xf
     pl.semaphore_wait(barrier, n - 1)
 
@@ -87,7 +99,7 @@
         t = t.astype(BF16).astype(F32)
         lane = lax.broadcasted_iota(jnp.int32, t.shape, 1)
         partner = jnp.where(lane % 64 < 32, _roll(t, LANES - 32), _roll(t, 32))
-        return t * cos_ref[...] + partner * sin_ref[...]
+        return t * rot_v[0] + partner * rot_v[1]
 
     def ship(dst, src, land, ssem, rsem):
         @pl.when(dst == me)
@@ -109,21 +121,23 @@
             w2_copy(s * (nm // ngrp) + i).start()
         a = a_v[...]
         q, k, v = (jnp.dot(a, wq_v[s, t], preferred_element_type=F32) for t in range(3))
-        vt = v.T.astype(BF16)
+        kr = [rope(k[:, j * LANES:(j + 1) * LANES]) for j in range(2)]
+        qr = [rope(q[:, j * LANES:(j + 1) * LANES]) for j in range(2)]
         for j in range(2):
-            cols = slice(j * LANES, (j + 1) * LANES)
-            kq = _pair(rope(k[:, cols]), rope(q[:, cols]))
-            for e in range(2):
-                h = 2 * j + e
-                send[4 * g + h, :r, :] = kq[e].astype(BF16)
+            for e, kk in enumerate(_pair(kr[j][:half], kr[j][half:])):
+                send[4 * g + 2 * j + e, :half, :] = kk.astype(BF16)
+        for at, t in ((half, jnp.concatenate(qr, axis=1)), (r, v)):
+            tt = t.T.astype(BF16)
+            for h in range(4):
                 for c in range(r // LANES):
-                    send[4 * g + h, r + c * dh:r + (c + 1) * dh, :] = vt[h * dh:(h + 1) * dh, c * LANES:(c + 1) * LANES]
+                    send[4 * g + h, at + c * dh:at + (c + 1) * dh, :] = tt[h * dh:(h + 1) * dh, c * LANES:(c + 1) * LANES]
         near = jnp.where(s == 0, odd, jnp.where(s == 1, 0, jnp.where(s == 2, 1, 1 - odd)))
         for i in range(4):
             ship(4 * g + 2 * (near + i // 2 - 2 * near * (i // 2)) + i % 2, send, recv, send_sem, recv_sem)
         return 0
 
     lax.fori_loop(0, ngrp, qkv_step, 0)
+    qt_v[:, dh:, :] = jnp.zeros((chips, LANES - dh, 2 * r), BF16)
     wo_copy.start()
 
     def mlp_step(i, _):
@@ -150,34 +164,27 @@
         return last
 
     def job(i, j, diag):
+        keys = [r * (h + 1) if diag else 2 * r for h in range(2)]
+        for h in range(2):
+            s_v[h, :keys[h], :] = jnp.dot(k_v[j, :keys[h], :], qt_v[i, :, h * r:(h + 1) * r], preferred_element_type=F32)
         for h in range(2):
             qi = 2 * i + h
-            halves = range(h + 1) if diag else range(2)
-            top = None
-            for g in halves:
-                sc = lax.dot_general(recv[2 * j + g, :r, :], qp_v[qi], (((1,), (1,)), ((), ())),
-                                     preferred_element_type=F32)
-                if diag and g == h:
-                    key = lax.broadcasted_iota(jnp.int32, sc.shape, 0)
-                    row = lax.broadcasted_iota(jnp.int32, sc.shape, 1)
-                    sc = jnp.where(key <= row, sc, NEG)
-                s_v[h, g] = sc
-                part = jnp.max(_transposed(sc), axis=0)
-                top = part if top is None else jnp.maximum(top, part)
-            top = jnp.max(top, axis=0, keepdims=True)
+            if diag:
+                sc = s_v[h, keys[h] - r:keys[h], :]
+                key = lax.broadcasted_iota(jnp.int32, sc.shape, 0)
+                row = lax.broadcasted_iota(jnp.int32, sc.shape, 1)
+                s_v[h, keys[h] - r:keys[h], :] = jnp.where(key <= row, sc, NEG)
+            top = jnp.max(jnp.max(_transposed(s_v[h, :keys[h], :]), axis=0), axis=0, keepdims=True)
             if not diag:
                 old = top_v[qi]
                 top = jnp.maximum(top, old)
                 alpha = jnp.exp2((old - top) * scale)
             top_v[qi] = top
-            den, out = None, None
-            for g in halves:
-                p = jnp.exp2(s_v[h, g] * scale - top * scale)
-                part = jnp.sum(_transposed(p), axis=0)
-                den = part if den is None else den + part
-                vt = jnp.concatenate([recv[2 * j + g, r + c * dh:r + (c + 1) * dh, :] for c in range(r // LANES)], axis=1)
-                part = jnp.dot(vt, p.astype(BF16), preferred_element_type=F32)
-                out = part if out is None else out + part
+            p = jnp.exp2(s_v[h, :keys[h], :] * scale - top * scale)
+            den = jnp.sum(_transposed(p), axis=0)
+            vt = jnp.concatenate([recv[2 * j + m // 2, r + (m % 2) * dh:r + (m % 2 + 1) * dh, :]
+                                  for m in range(keys[h] // LANES)], axis=1)
+            out = jnp.dot(vt, p.astype(BF16), preferred_element_type=F32)
             if not diag:
                 den = den_v[qi] * alpha + den
                 out = out_v[qi] * alpha + out
@@ -197,25 +204,39 @@
         b = order(t)
         for h in range(2):
             pltpu.make_async_copy(send.at[2 * b + h], recv.at[2 * b + h], recv_sem.at[2 * b + h]).wait()
-            kq = recv[2 * b + h, :r, :].astype(F32)
-            qp_v[2 * b + h] = jnp.where(_low(kq.shape), _roll(kq, dh), 0.0).astype(BF16)
+            k_v[b, h * r:h * r + half, :] = recv[2 * b + h, :half, :]
+            k_v[b, h * r + half:(h + 1) * r, :] = _roll(recv[2 * b + h, :half, :].astype(F32), dh).astype(BF16)
+            for c in range(r // LANES):
+                qt_v[b, :dh, h * r + c * LANES:h * r + (c + 1) * LANES] = recv[2 * b + h, half + c * dh:half + (c + 1) * dh, :]
         job(b, b, True)
 
-        def pairs(u, _):
-            c = order(t - 1 - u)
-            i = jnp.maximum(b, c)
-            job(i, jnp.minimum(b, c), False)
-
-            @pl.when((i != b) & (ready(i) == t))
+        def before(u, _):
+            c = order(u)
+
+            @pl.when(c < b)
             def _():
-                finish(i)
+                job(b, c, False)
             return 0
 
-        lax.fori_loop(0, t, pairs, 0)
+        lax.fori_loop(0, t, before, 0)
 
         @pl.when(ready(b) == t)
         def _():
             finish(b)
+
+        def after(u, _):
+            c = order(t - 1 - u)
+
+            @pl.when(c > b)
+            def _():
+                job(c, b, False)
+
+            @pl.when((c > b) & (ready(c) == t))
+            def _():
+                finish(c)
+            return 0
+
+        lax.fori_loop(0, t, after, 0)
         return 0
 
     lax.fori_loop(0, chips, attend, 0)
@@ -231,7 +252,8 @@
     wo_copy.wait()
     for c in range(d // 256):
         cols = slice(c * 256, (c + 1) * 256)
-        y_ref[:, cols] = (acc_v[:, cols] + jnp.dot(o_v[...], wo_v[:, cols], preferred_element_type=F32)).astype(BF16)
+        y_v[:, cols] = (acc_v[:, cols] + jnp.dot(o_v[...], wo_v[:, cols], preferred_element_type=F32)).astype(BF16)
+        pltpu.make_async_copy(y_v.at[:, cols], y_ref.at[:, cols], y_sem.at[c]).start()
 
     def drained(i, _):
         @pl.when(i != me)
@@ -241,14 +263,20 @@
         return 0
 
     lax.fori_loop(0, n, drained, 0)
-
-
-def _tables(pos, dh):
-    half = dh // 2
-    inv = 10000.0 ** (-2.0 * jnp.arange(half, dtype=F32) / dh)
-    ang = pos.astype(F32)[:, None] * inv[None, :]
-    cos, sin = jnp.cos(ang), jnp.sin(ang)
-    return jnp.concatenate([cos] * 4, axis=1), jnp.concatenate([-sin, sin, -sin, sin], axis=1)
+    for c in range(d // 256):
+        cols = slice(c * 256, (c + 1) * 256)
+        pltpu.make_async_copy(y_v.at[:, cols], y_ref.at[:, cols], y_sem.at[c]).wait()
+
+
+def _tables(r, n, dh):
+    inv = 10000.0 ** (-2.0 * np.arange(dh // 2) / dh)
+    sign = np.array([-1.0, 1.0, -1.0, 1.0]).repeat(dh // 2)
+
+    def both(pos):
+        ang = np.tile(pos[:, None] * inv[None, :], (1, 4))
+        return np.stack([np.cos(ang), np.sin(ang) * sign]).astype(np.float32)
+
+    return both(np.arange(r)), both(np.arange(n) * r)
 
 
 def solution(mesh):
@@ -259,22 +287,24 @@
         nh, dh, _ = wo.shape
         f = w1.shape[1]
         assert nh == n and dh * 2 == LANES and r == 256
-        cos, sin = _tables(lax.axis_index("seq") * r + jnp.arange(r), dh)
+        turn, base = _tables(r, n, dh)
         nm, ngrp, chunk = f // HCOL, n // 4, r + r // 2
-        vm = pl.BlockSpec(memory_space=pltpu.VMEM)
         hbm = pl.BlockSpec(memory_space=pl.ANY)
         dma = pltpu.SemaphoreType.DMA
         return pl.pallas_call(
             functools.partial(_kernel, n, dh ** -0.5 * math.log2(math.e)),
             out_shape=jax.ShapeDtypeStruct((r, d), BF16),
-            in_specs=[vm] * 7 + [hbm] * 4,
-            out_specs=vm,
+            in_specs=[hbm] * 11,
+            out_specs=hbm,
             scratch_shapes=[
+                pltpu.VMEM((r, d), BF16), pltpu.VMEM((4, 1, d), F32), pltpu.VMEM(turn.shape, F32),
+                pltpu.VMEM(base.shape, F32), pltpu.VMEM(turn.shape, F32), pltpu.VMEM((r, d), BF16), dma((7,)), dma((d // 256,)),
                 pltpu.VMEM((ngrp, 3, d, d // ngrp), BF16), pltpu.VMEM((d, d), BF16),
                 pltpu.VMEM((nm, d, HCOL), BF16), pltpu.VMEM((nm, HCOL, d), BF16),
                 pltpu.VMEM((r, d), BF16), pltpu.VMEM((r, d), BF16), pltpu.VMEM((r, d), F32),
                 pltpu.VMEM((n, chunk, LANES), BF16), pltpu.VMEM((n, chunk, LANES), BF16),
-                pltpu.VMEM((n, r, LANES), BF16), pltpu.VMEM((2, 2, r, r), F32),
+                pltpu.VMEM((n // 2, 2 * r, LANES), BF16), pltpu.VMEM((n // 2, LANES, 2 * r), BF16),
+                pltpu.VMEM((2, 2 * r, r), F32),
                 pltpu.VMEM((n, 1, r), F32), pltpu.VMEM((n, 8, r), F32), pltpu.VMEM((n, dh, r), F32),
                 pltpu.VMEM((n, r // 2, LANES), BF16), pltpu.VMEM((n, r // 2, LANES), BF16),
                 pltpu.VMEM((r, d), BF16),
@@ -284,7 +314,7 @@
             compiler_params=pltpu.CompilerParams(
                 collective_id=0, has_side_effects=True, vmem_limit_bytes=62 * 2 ** 20),
             name="layer",
-        )(x, g1[None], b1[None], g2[None], b2[None], cos, sin, wqkv, wo.reshape(nh * dh, d), w1, w2)
+        )(x, g1[None], b1[None], g2[None], b2[None], turn, base, wqkv, wo.reshape(nh * dh, d), w1, w2)
 
     rows = P(("data", "seq"), None)
     rep = P()

time: 75.5 us -> 67.7 us (0.90)
  the two profiles are of different devices: /device:TPU:127 before, /device:TPU:95 now
where the time goes in v2:
time: 67.7 us; the launch traced here: 67.6 us
  Pallas kernels  65.7 us (97%)
  local copies, waits for them, and re-layouts  1.87 us (3%)
    pallas_call x1, Pallas kernels, local(): pl.pallas_call(functools.partial(_kernel, n, dh ** (-0.5) * math.log2(mat...  65.7 us
    unnamed x1, local copies, waits for them, and re-layouts  1.87 us

profile of v2, /device:TPU:95, one launch (start us, length us, event | category | flops | bytes accessed | tf_op | source)
XLA Modules:
  0.0 67.6 jit_solution(3594037913407207778)
XLA Ops:
  0.0 65.7 %layer.1 = bf16[256,1024]{1,0:T(8,128)(2,1)} custom-call(bf16[256,1024]{1,0:T(8,128)(2,1)} %x_ref.1, f32[1,1024]{1,0:T(1,128)} %bitcast.6, f32[1,1024]{1,0:T(1,128)} %bitcast.7, f32[1,1024]{1,0:T(1,128)} %bitcast.8, f32[1,1024]{1,0:T(1,128)} %bitcast.9, f32[2,256,128]{2,1,0:T(8,128)} %constant.4.clone.turn_ref, f32[2,16,128]{2,1,0:T(8,128)} %constant.5.clone.base_ref, ...), custom_call_target="tpu_custom_call" | custom-call | tf_op jit(solution)/shard_map/layer/pallas_call | solution.py:294
  65.8 1.9 %copy.13 = bf16[256,1024]{1,0:T(8,128)(2,1)} copy(bf16[256,1024]{1,0:T(8,128)(2,1)} %layer.1) | data formatting | bytes 1048576

commit v3 on v2

--- a/solution.py
+++ b/solution.py
@@ -35,11 +35,12 @@
 
 
 def _kernel(n, scale, x_ref, g1_ref, b1_ref, g2_ref, b2_ref, turn_ref, base_ref, wqkv_ref, wo_ref, w1_ref, w2_ref, y_ref,
-            x_v, gb_v, turn_v, base_v, rot_v, y_v, in_sem, y_sem, wq_v, wo_v, w1_v, w2_v, a_v, m_v, acc_v, send, recv, k_v, qt_v, s_v, top_v, den_v, out_v, o_send, o_recv, o_v,
+            x_v, gb_v, turn_v, base_v, rot_v, y_v, in_sem, y_sem, wq_v, wo_v, w1_v, w2_v, a_v, m_v, acc_v, send, recv, k_v, qt_v, s0_v, s1_v, peak0_v, peak1_v, top_v, den_v, out_v, o_send, o_recv, o_v,
             wq_sem, wo_sem, w1_sem, w2_sem, send_sem, recv_sem, osend_sem, orecv_sem):
     r, d = x_v.shape
     dh = LANES // 2
     half = r // 2
+    slots = ((s0_v, peak0_v), (s1_v, peak1_v))
     chips = n // 2
     ngrp = n // 4
     gcol = d // ngrp
@@ -163,33 +164,45 @@
             last = jnp.where(j <= i, jnp.maximum(last, place(j)), last)
         return last
 
-    def job(i, j, diag):
-        keys = [r * (h + 1) if diag else 2 * r for h in range(2)]
-        for h in range(2):
-            s_v[h, :keys[h], :] = jnp.dot(k_v[j, :keys[h], :], qt_v[i, :, h * r:(h + 1) * r], preferred_element_type=F32)
+    def score(i, j, slot):
+        s_v, peak_v = slots[slot]
+        for h in range(2):
+            sc = jnp.dot(k_v[j], qt_v[i, :, h * r:(h + 1) * r], preferred_element_type=F32)
+            s_v[h] = sc
+            peak_v[h] = jnp.max(_transposed(sc), axis=0)
+
+    def absorb(i, j, slot):
+        s_v, peak_v = slots[slot]
         for h in range(2):
             qi = 2 * i + h
-            if diag:
-                sc = s_v[h, keys[h] - r:keys[h], :]
-                key = lax.broadcasted_iota(jnp.int32, sc.shape, 0)
-                row = lax.broadcasted_iota(jnp.int32, sc.shape, 1)
-                s_v[h, keys[h] - r:keys[h], :] = jnp.where(key <= row, sc, NEG)
-            top = jnp.max(jnp.max(_transposed(s_v[h, :keys[h], :]), axis=0), axis=0, keepdims=True)
-            if not diag:
-                old = top_v[qi]
-                top = jnp.maximum(top, old)
-                alpha = jnp.exp2((old - top) * scale)
+            old = top_v[qi]
+            top = jnp.maximum(jnp.max(peak_v[h], axis=0, keepdims=True), old)
+            alpha = jnp.exp2((old - top) * scale)
             top_v[qi] = top
-            p = jnp.exp2(s_v[h, :keys[h], :] * scale - top * scale)
-            den = jnp.sum(_transposed(p), axis=0)
-            vt = jnp.concatenate([recv[2 * j + m // 2, r + (m % 2) * dh:r + (m % 2 + 1) * dh, :]
-                                  for m in range(keys[h] // LANES)], axis=1)
-            out = jnp.dot(vt, p.astype(BF16), preferred_element_type=F32)
-            if not diag:
-                den = den_v[qi] * alpha + den
-                out = out_v[qi] * alpha + out
-            den_v[qi] = den
-            out_v[qi] = out
+            p = jnp.exp2(s_v[h] * scale - top * scale)
+            den_v[qi] = den_v[qi] * alpha + jnp.sum(_transposed(p), axis=0)
+            out_v[qi] = out_v[qi] * alpha + jnp.dot(values(j, 2 * r), p.astype(BF16), preferred_element_type=F32)
+
+    def values(j, nk):
+        return jnp.concatenate([recv[2 * j + m // 2, r + (m % 2) * dh:r + (m % 2 + 1) * dh, :]
+                                for m in range(nk // LANES)], axis=1)
+
+    def diagonal(i, slot):
+        s_v, _ = slots[slot]
+        for h in range(2):
+            qi, nk = 2 * i + h, (h + 1) * r
+            s_v[h, :nk, :] = jnp.dot(k_v[i, :nk, :], qt_v[i, :, h * r:(h + 1) * r], preferred_element_type=F32)
+            sc = s_v[h, nk - r:nk, :]
+            key = lax.broadcasted_iota(jnp.int32, sc.shape, 0)
+            row = lax.broadcasted_iota(jnp.int32, sc.shape, 1)
+            s_v[h, nk - r:nk, :] = jnp.where(key <= row, sc, NEG)
+        for h in range(2):
+            qi, nk = 2 * i + h, (h + 1) * r
+            top = jnp.max(jnp.max(_transposed(s_v[h, :nk, :]), axis=0), axis=0, keepdims=True)
+            top_v[qi] = top
+            p = jnp.exp2(s_v[h, :nk, :] * scale - top * scale)
+            den_v[qi] = jnp.sum(_transposed(p), axis=0)
+            out_v[qi] = jnp.dot(values(i, nk), p.astype(BF16), preferred_element_type=F32)
 
     def finish(i):
         for h in range(2):
@@ -208,35 +221,47 @@
             k_v[b, h * r + half:(h + 1) * r, :] = _roll(recv[2 * b + h, :half, :].astype(F32), dh).astype(BF16)
             for c in range(r // LANES):
                 qt_v[b, :dh, h * r + c * LANES:h * r + (c + 1) * LANES] = recv[2 * b + h, half + c * dh:half + (c + 1) * dh, :]
-        job(b, b, True)
-
-        def before(u, _):
-            c = order(u)
-
-            @pl.when(c < b)
+        less = jnp.where(t % 2 == 1, jnp.minimum(b, t), jnp.maximum(b + t + 1 - chips, 0))
+
+        def pick(v):
+            v = jnp.maximum(jnp.minimum(v, t - 1), 0)
+            return (jnp.where(t % 2 == 1, b + chips - 1 - v, b + t - v)) % chips
+
+        def ahead(v, slot):
+            c = pick(v)
+            score(jnp.maximum(b, c), jnp.minimum(b, c), slot)
+
+        def take(v, slot):
+            c = pick(v)
+            absorb(jnp.maximum(b, c), jnp.minimum(b, c), slot)
+
+        def settle(v):
+            row = jnp.maximum(b, pick(v))
+
+            @pl.when(((row != b) | (v + 1 == less)) & (ready(row) == t))
             def _():
-                job(b, c, False)
-            return 0
-
-        lax.fori_loop(0, t, before, 0)
-
-        @pl.when(ready(b) == t)
+                finish(row)
+
+        ahead(0, 0)
+        diagonal(b, 1)
+
+        @pl.when((less == 0) & (ready(b) == t))
         def _():
             finish(b)
 
-        def after(u, _):
-            c = order(t - 1 - u)
-
-            @pl.when(c > b)
+        def pairs(m, _):
+            ahead(2 * m + 1, 1)
+            take(2 * m, 0)
+            settle(2 * m)
+
+            @pl.when(2 * m + 1 < t)
             def _():
-                job(c, b, False)
-
-            @pl.when((c > b) & (ready(c) == t))
-            def _():
-                finish(c)
+                ahead(2 * m + 2, 0)
+                take(2 * m + 1, 1)
+                settle(2 * m + 1)
             return 0
 
-        lax.fori_loop(0, t, after, 0)
+        lax.fori_loop(0, (t + 1) // 2, pairs, 0)
         return 0
 
     lax.fori_loop(0, chips, attend, 0)
@@ -304,7 +329,8 @@
                 pltpu.VMEM((r, d), BF16), pltpu.VMEM((r, d), BF16), pltpu.VMEM((r, d), F32),
                 pltpu.VMEM((n, chunk, LANES), BF16), pltpu.VMEM((n, chunk, LANES), BF16),
                 pltpu.VMEM((n // 2, 2 * r, LANES), BF16), pltpu.VMEM((n // 2, LANES, 2 * r), BF16),
-                pltpu.VMEM((2, 2 * r, r), F32),
+                pltpu.VMEM((2, 2 * r, r), F32), pltpu.VMEM((2, 2 * r, r), F32),
+                pltpu.VMEM((2, 8, r), F32), pltpu.VMEM((2, 8, r), F32),
                 pltpu.VMEM((n, 1, r), F32), pltpu.VMEM((n, 8, r), F32), pltpu.VMEM((n, dh, r), F32),
                 pltpu.VMEM((n, r // 2, LANES), BF16), pltpu.VMEM((n, r // 2, LANES), BF16),
                 pltpu.VMEM((r, d), BF16),

time: 67.7 us -> 65.8 us (0.972)
  Pallas kernels: 65.7 us -> 63.8 us
    pallas_call x1, Pallas kernels: 65.7 us -> 63.8 us  [local(): pl.pallas_call(functools.partial(_kernel, n, dh ** (-0.5) * math.log2(mat...]
where the time goes in v3:
time: 65.8 us; the launch traced here: 65.7 us
  Pallas kernels  63.8 us (97%)
  local copies, waits for them, and re-layouts  1.87 us (3%)
    pallas_call x1, Pallas kernels, local(): pl.pallas_call(functools.partial(_kernel, n, dh ** (-0.5) * math.log2(mat...  63.8 us
    unnamed x1, local copies, waits for them, and re-layouts  1.87 us

profile of v3, /device:TPU:95, one launch (start us, length us, event | category | flops | bytes accessed | tf_op | source)
XLA Modules:
  0.0 65.7 jit_solution(17900976086531672622)
XLA Ops:
  0.0 63.8 %layer.1 = bf16[256,1024]{1,0:T(8,128)(2,1)} custom-call(bf16[256,1024]{1,0:T(8,128)(2,1)} %x_ref.1, f32[1,1024]{1,0:T(1,128)} %bitcast.6, f32[1,1024]{1,0:T(1,128)} %bitcast.7, f32[1,1024]{1,0:T(1,128)} %bitcast.8, f32[1,1024]{1,0:T(1,128)} %bitcast.9, f32[2,256,128]{2,1,0:T(8,128)} %constant.4.clone.turn_ref, f32[2,16,128]{2,1,0:T(8,128)} %constant.5.clone.base_ref, ...), custom_call_target="tpu_custom_call" | custom-call | tf_op jit(solution)/shard_map/layer/pallas_call | solution.py:319
  63.8 1.9 %copy.13 = bf16[256,1024]{1,0:T(8,128)(2,1)} copy(bf16[256,1024]{1,0:T(8,128)(2,1)} %layer.1) | data formatting | bytes 1048576

commit v4 on v3

--- a/solution.py
+++ b/solution.py
@@ -77,7 +77,7 @@
 
     wo_copy = pltpu.make_async_copy(wo_ref, wo_v, wo_sem)
 
-    for s in range(ngrp):
+    for s in range(2):
         for t in range(3):
             wq_copy(s, t).start()
 
@@ -94,7 +94,6 @@
     a_v[...] = (xn * gb_v[0] + gb_v[1]).astype(BF16)
     m_v[...] = (xn * gb_v[2] + gb_v[3]).astype(BF16)
     acc_v[...] = xf
-    pl.semaphore_wait(barrier, n - 1)
 
     def rope(t):
         t = t.astype(BF16).astype(F32)
@@ -117,6 +116,12 @@
         g = group(s)
         for t in range(3):
             wq_copy(s, t).wait()
+
+        @pl.when(s + 2 < ngrp)
+        def _():
+            for t in range(3):
+                wq_copy(s + 2, t).start()
+
         for i in range(nm // ngrp):
             w1_copy(s * (nm // ngrp) + i).start()
             w2_copy(s * (nm // ngrp) + i).start()
@@ -132,6 +137,9 @@
             for h in range(4):
                 for c in range(r // LANES):
                     send[4 * g + h, at + c * dh:at + (c + 1) * dh, :] = tt[h * dh:(h + 1) * dh, c * LANES:(c + 1) * LANES]
+        @pl.when(s == 0)
+        def _():
+            pl.semaphore_wait(barrier, n - 1)
         near = jnp.where(s == 0, odd, jnp.where(s == 1, 0, jnp.where(s == 2, 1, 1 - odd)))
         for i in range(4):
             ship(4 * g + 2 * (near + i // 2 - 2 * near * (i // 2)) + i % 2, send, recv, send_sem, recv_sem)

time: 65.8 us -> 64.6 us (0.982)
  Pallas kernels: 63.8 us -> 62.5 us
    pallas_call x1, Pallas kernels: 63.8 us -> 62.5 us  [local(): pl.pallas_call(functools.partial(_kernel, n, dh ** (-0.5) * math.log2(mat...]
where the time goes in v4:
time: 64.6 us; the launch traced here: 64.3 us
  Pallas kernels  62.5 us (97%)
  local copies, waits for them, and re-layouts  1.87 us (3%)
    pallas_call x1, Pallas kernels, local(): pl.pallas_call(functools.partial(_kernel, n, dh ** (-0.5) * math.log2(mat...  62.5 us
    unnamed x1, local copies, waits for them, and re-layouts  1.87 us

profile of v4, /device:TPU:95, one launch (start us, length us, event | category | flops | bytes accessed | tf_op | source)
XLA Modules:
  0.0 64.3 jit_solution(7959249355058753361)
XLA Ops:
  0.0 62.5 %layer.1 = bf16[256,1024]{1,0:T(8,128)(2,1)} custom-call(bf16[256,1024]{1,0:T(8,128)(2,1)} %x_ref.1, f32[1,1024]{1,0:T(1,128)} %bitcast.6, f32[1,1024]{1,0:T(1,128)} %bitcast.7, f32[1,1024]{1,0:T(1,128)} %bitcast.8, f32[1,1024]{1,0:T(1,128)} %bitcast.9, f32[2,256,128]{2,1,0:T(8,128)} %constant.4.clone.turn_ref, f32[2,16,128]{2,1,0:T(8,128)} %constant.5.clone.base_ref, ...), custom_call_target="tpu_custom_call" | custom-call | tf_op jit(solution)/shard_map/layer/pallas_call | solution.py:327
  62.5 1.9 %copy.13 = bf16[256,1024]{1,0:T(8,128)(2,1)} copy(bf16[256,1024]{1,0:T(8,128)(2,1)} %layer.1) | data formatting | bytes 1048576
